TPU v7x, 32 devices: a whole 2x2x4 slice. The times are simulated.
32 devices in a mesh: dp: 4 (over z), ctx: 8 (over y, x, core).
Axes of the slice: x: 2, y: 2, z: 4, core: 2. Of those that a mesh axis runs over, the one named last changes fastest.
Arguments:
- queries: bfloat16 [4, 1024, 4096], P('dp', 'ctx'), may hold values from -120 to 120
- layer_input: bfloat16 [4, 1024, 4096], P('dp', 'ctx'), may hold values from -6 to 6
- key_value_weight: bfloat16 [4096, 1024], P(('dp', 'ctx')), may hold values from -0.25 to 0.25
- output_gradient: bfloat16 [4, 1024, 4096], P('dp', 'ctx'), may hold values from -6 to 6
- document_lengths: int32 [4, 8], P('dp'), may hold values from 1 to 256, 1024 in all within a row
Outputs:
- attended: bfloat16 [4, 1024, 4096], P('dp', 'ctx')
- query_grad: bfloat16 [4, 1024, 4096], P('dp', 'ctx')
- input_grad: bfloat16 [4, 1024, 4096], P('dp', 'ctx')
Inputs may be any that keep to these rules, and one draw needn't show every extreme that they name: `document_lengths`: each row holds the lengths of the 8 documents of one sequence in order; they sum to 1024, and one of them is exactly 256.
All inputs are finite; a program needn't handle non-finite values.
Results may differ from a plain program's by a relative error of at most 0.02.
The roundings to bfloat16 on the way count: a program that leaves them out, or rounds other values in their place, can miss the bound.
Values may be sent and summed in bfloat16 or wider, within the bound.
No kernel may reach another device: no remote copies, remote signals or barrier semaphores. Data moves between devices by JAX's collectives and lax.ppermute only.
A program may use at most 128 MiB of HBM per device.

v0:
```python
import functools
import math

import jax
import jax.numpy as jnp
from jax import lax
from jax.experimental import pallas as pl
from jax.experimental.pallas import tpu as pltpu
from jax.sharding import PartitionSpec as P


QUERY_HEADS = 32
KEY_VALUE_HEADS = 4
HEAD_SIZE = 128
HEAD_GROUP = QUERY_HEADS // KEY_VALUE_HEADS
HALF = KEY_VALUE_HEADS * HEAD_SIZE
CHUNK_HEADS = 2
CHUNKS = KEY_VALUE_HEADS // CHUNK_HEADS
AXES = ("dp", "ctx")
NEGATIVE = -1e30


VMEM = pl.BlockSpec(memory_space=pltpu.VMEM)
SMEM = pl.BlockSpec(memory_space=pltpu.SMEM)
HBM = pl.BlockSpec(memory_space=pltpu.HBM)
NT = (((1,), (1,)), ((), ()))


def params(mib):
    return pltpu.CompilerParams(vmem_limit_bytes=mib * 1024 * 1024)


def cost(flops, moved):
    return pl.CostEstimate(flops=flops, bytes_accessed=moved, transcendentals=0)


def inside(value):
    return pltpu.with_memory_space_constraint(value, pltpu.VMEM)


def outside(value):
    return pltpu.with_memory_space_constraint(value, pltpu.HBM)


def columns(index):
    return pl.ds(pl.multiple_of(index * 128, 128), 128)


def shard_of(depth, across, core, block):
    z = lax.axis_index("dp")
    place = lax.axis_index("ctx")
    source = z - block // 4
    source = jnp.where(source < 0, source + depth, source)
    place = place - 2 * (place % 2) * core + core
    flip = block % 4
    if flip & 1:
        place = place + 2 - 4 * ((place // 2) % 2)
    if flip & 2:
        place = place + 4 - 8 * ((place // 4) % 2)
    return source * across + place


def arrange_kernel(sizes, x_ref, y_ref, out_ref):
    rows = x_ref.shape[0]
    for j in range(out_ref.shape[1] // 128):
        place = slice(j * 128, (j + 1) * 128)
        shard = shard_of(*sizes, 0, j)
        out_ref[:rows, place] = x_ref[:, columns(shard)]
        out_ref[rows:, place] = y_ref[:, columns(shard)]


def arrange(sizes, mine, other):
    rows, width = mine.shape
    return pl.pallas_call(
        functools.partial(arrange_kernel, sizes),
        out_shape=pltpu.VMEM((2 * rows, width // 2), mine.dtype),
        in_specs=[VMEM, VMEM],
        out_specs=VMEM,
        compiler_params=params(16),
        cost_estimate=cost(1 << 20, 3 << 20),
        name="arrange",
    )(mine, inside(other))


def fetch_kernel(count, *refs):
    sems = refs[-1]
    moves = [pltpu.make_async_copy(refs[j], refs[count + j], sems.at[j]) for j in range(count)]
    for move in moves:
        move.start()
    for move in moves:
        move.wait()


def fetch(*values):
    count = len(values)
    return pl.pallas_call(
        functools.partial(fetch_kernel, count),
        out_shape=[pltpu.VMEM(value.shape, value.dtype) for value in values],
        in_specs=[HBM] * count,
        out_specs=[VMEM] * count,
        scratch_shapes=[pltpu.SemaphoreType.DMA((count,))],
        compiler_params=params(16),
        cost_estimate=cost(1 << 20, 4 << 20),
        name="fetch",
    )(*[outside(value) for value in values])


def project_kernel(slot, count, last, x_ref, *refs):
    refs = list(refs)
    if slot:
        acc_ref = refs.pop(0)
    pieces = [refs.pop(0) for _ in range(count)]
    packed_ref = refs.pop(0)
    outs = refs
    rows = x_ref[:, slice(slot * 512, (slot + 1) * 512)]
    half = rows.shape[0] // 2
    for n in range(0, 2 * HALF, 256):
        side = 0 if n < HALF else 1
        cut = slice(n, n + 256)
        part = slice(n - side * HALF, n - side * HALF + 256)
        blocks = [ref[:, cut] for ref in pieces[:3]]
        blocks.append(pieces[3][:, cut] if count == 4 else pieces[3 + side][:, part])
        weight = jnp.concatenate(blocks, axis=0)
        packed_ref[:, cut] = weight
        total = jnp.dot(rows, weight, preferred_element_type=jnp.float32)
        if slot:
            total = total + acc_ref[:, cut]
        if last:
            outs[0][:, cut] = total[:half]
            outs[1][:, cut] = total[half:]
        else:
            outs[0][:, cut] = total


def project(slot, x, acc, pieces, last):
    rows = x.shape[0] // 2
    out = [pltpu.VMEM((rows, 2 * HALF), jnp.float32)] * 2
    if not last:
        out = [pltpu.VMEM((2 * rows, 2 * HALF), jnp.float32)]
    given = [inside(x)] + ([] if slot == 0 else [inside(acc)])
    given += list(pieces[:1] if slot == 0 else []) + [inside(piece) for piece in pieces[0 if slot else 1 :]]
    outs = pl.pallas_call(
        functools.partial(project_kernel, slot, len(pieces), last),
        out_shape=[pltpu.VMEM((512, 2 * HALF), jnp.bfloat16)] + out,
        in_specs=[VMEM] * len(given),
        out_specs=[VMEM] * (len(out) + 1),
        compiler_params=params(16),
        cost_estimate=cost(4 * rows * 512 * 2 * HALF, 4 << 20),
        name="project",
    )(*given)
    return outs[0], outs[1:]


def join_kernel(a_ref, b_ref, *outs):
    cut = CHUNK_HEADS * HEAD_SIZE
    for c, out in enumerate(outs):
        for side in range(2):
            span = slice(side * HALF + c * cut, side * HALF + (c + 1) * cut)
            out[:, side * cut : (side + 1) * cut] = (a_ref[:, span] + b_ref[:, span]).astype(out.dtype)


def join(mine, other):
    rows = mine.shape[0]
    return pl.pallas_call(
        join_kernel,
        out_shape=[pltpu.VMEM((rows, 2 * CHUNK_HEADS * HEAD_SIZE), jnp.bfloat16)] * CHUNKS,
        in_specs=[VMEM, VMEM],
        out_specs=[VMEM] * CHUNKS,
        compiler_params=params(16),
        cost_estimate=cost(1 << 20, 2 << 20),
        name="join",
    )(inside(mine), inside(other))


def attend_kernel(chunk, reach, lengths_ref, q_ref, g_ref, *refs):
    refs = list(refs)
    kv = [refs.pop(0) for _ in range(reach + 1)]
    o_ref, dq_ref = refs[0], refs[1]
    parts = refs[2 : 3 + reach]
    bias_ref, score_ref, press_ref, w_ref, p_ref, s_ref = refs[3 + reach :]
    rows = q_ref.shape[0]
    share = o_ref.shape[1]
    window = (reach + 1) * rows
    start = lax.axis_index("ctx") * rows
    key_pos = start - reach * rows + lax.broadcasted_iota(jnp.int32, (window, rows), 0)
    query_pos = start + lax.broadcasted_iota(jnp.int32, (8, rows), 1)
    key_doc = jnp.zeros((window, rows), jnp.int32)
    query_doc = jnp.zeros((8, rows), jnp.int32)
    end = jnp.int32(0)
    for document in range(lengths_ref.shape[1]):
        end = end + lengths_ref[0, document]
        key_doc = key_doc + (key_pos >= end).astype(jnp.int32)
        query_doc = query_doc + (query_pos >= end).astype(jnp.int32)
    allowed = (key_doc == query_doc[:1]) & (key_pos <= query_pos[:1]) & (key_pos >= 0)
    bias_ref[...] = jnp.where(allowed, 0.0, NEGATIVE)
    scale = 1.0 / math.sqrt(HEAD_SIZE)
    factor = scale * math.log2(math.e)
    size = HEAD_GROUP * rows
    for head in range(CHUNK_HEADS):
        k_cut = slice(head * HEAD_SIZE, (head + 1) * HEAD_SIZE)
        v_cut = slice((CHUNK_HEADS + head) * HEAD_SIZE, (CHUNK_HEADS + head + 1) * HEAD_SIZE)
        keys = jnp.concatenate([kv[reach - j][:, k_cut] for j in range(reach + 1)], axis=0)
        values = jnp.concatenate([kv[reach - j][:, v_cut] for j in range(reach + 1)], axis=0)
        keys_t = keys.T
        values_t = values.T
        base = head * HEAD_GROUP * HEAD_SIZE
        outs = [slice(base + j * HEAD_SIZE, base + (j + 1) * HEAD_SIZE) for j in range(HEAD_GROUP)]
        cuts = [slice(cut.start + chunk * share, cut.stop + chunk * share) for cut in outs]
        mine = slice(head * size, (head + 1) * size)
        q_all = jnp.concatenate([q_ref[:, cut] for cut in cuts], axis=0)
        g_all = jnp.concatenate([g_ref[:, cut] for cut in cuts], axis=0)
        score_ref[:, mine] = lax.dot_general(keys, q_all, NT, preferred_element_type=jnp.float32)
        press_ref[:, mine] = lax.dot_general(values, g_all, NT, preferred_element_type=jnp.float32)
        inverses = []
        for j in range(HEAD_GROUP):
            spot = slice(head * size + j * rows, head * size + (j + 1) * rows)
            score = score_ref[:, spot] + bias_ref[...]
            top = jnp.max(score, axis=0, keepdims=True)
            weight = jnp.exp2((score - top) * factor)
            inverse = 1.0 / jnp.sum(weight, axis=0, keepdims=True)
            inverses.append(inverse)
            w_ref[:, spot] = weight.astype(jnp.bfloat16)
            prob = weight * inverse
            p_ref[:, spot] = prob.astype(jnp.bfloat16)
            product = jnp.sum(prob * press_ref[:, spot], axis=0, keepdims=True)
            s_ref[:, spot] = (prob * (press_ref[:, spot] - product)).astype(jnp.bfloat16)
        mixed = jnp.dot(values_t, w_ref[:, mine], preferred_element_type=jnp.float32)
        mixed = (mixed * jnp.concatenate(inverses, axis=1)).astype(jnp.bfloat16)
        dq = jnp.dot(keys_t, s_ref[:, mine], preferred_element_type=jnp.float32)
        dq = (dq * scale).astype(jnp.bfloat16)
        for j, cut in enumerate(outs):
            o_ref[:, cut] = mixed[:, j * rows : (j + 1) * rows].T
            dq_ref[:, cut] = dq[:, j * rows : (j + 1) * rows].T
        for j in range(reach + 1):
            span = slice((reach - j) * rows, (reach - j + 1) * rows)
            dk = jnp.dot(s_ref[span, mine], q_all, preferred_element_type=jnp.float32) * scale
            dv = jnp.dot(p_ref[span, mine], g_all, preferred_element_type=jnp.float32)
            parts[j][:, k_cut] = dk.astype(parts[j].dtype)
            parts[j][:, v_cut] = dv.astype(parts[j].dtype)


def attend(lengths, queries, gradient, kv, chunk):
    rows, width = queries.shape
    reach = len(kv) - 1
    share = width // CHUNKS
    window = (reach + 1) * rows
    given = [lengths] + [inside(value) for value in (queries, gradient, *kv)]
    whole = pltpu.VMEM((rows, share), jnp.bfloat16)
    piece = (rows, 2 * CHUNK_HEADS * HEAD_SIZE)
    size = CHUNK_HEADS * HEAD_GROUP * rows
    outs = pl.pallas_call(
        functools.partial(attend_kernel, chunk, reach),
        out_shape=[whole, whole]
        + [pltpu.VMEM(piece, jnp.float32 if j == 0 else jnp.bfloat16) for j in range(reach + 1)],
        in_specs=[SMEM] + [VMEM] * (reach + 3),
        out_specs=[VMEM] * (reach + 3),
        scratch_shapes=[
            pltpu.VMEM((window, rows), jnp.float32),
            pltpu.VMEM((window, size), jnp.float32),
            pltpu.VMEM((window, size), jnp.float32),
            pltpu.VMEM((window, size), jnp.bfloat16),
            pltpu.VMEM((window, size), jnp.bfloat16),
            pltpu.VMEM((window, size), jnp.bfloat16),
        ],
        compiler_params=params(min(60, 14 + 14 * window * size // (1 << 20))),
        cost_estimate=cost(12 * rows * window * share * 2, 4 << 20),
        name="attend",
    )(*given)
    return outs[:2], outs[2:]


def finish_kernel(sizes, chunk, terms, slots, extra, *refs):
    refs = list(refs)
    parts = [refs.pop(0) for _ in range(terms)]
    if chunk:
        acc_ref = refs.pop(0)
    halves = [[refs.pop(0) for _ in range(slots)] for _ in range(2)]
    results = [refs.pop(0) for _ in range(extra)]
    out_ref = refs.pop(0)
    last = chunk + 1 == CHUNKS
    moves = []
    if extra:
        sems = refs.pop()
        for j, ref in enumerate(results):
            share = ref.shape[1]
            spot = slice((j // 2) * share, (j // 2 + 1) * share)
            moves.append(pltpu.make_async_copy(ref, refs[j % 2].at[:, spot], sems.at[j]))
            moves[-1].start()
    if last:
        staged_ref, out_sems = refs
    cut = CHUNK_HEADS * HEAD_SIZE
    total = parts[0][...]
    for part in parts[1:]:
        total = total + part[...].astype(jnp.float32)
    flat = total.astype(jnp.bfloat16)
    near_cut = slice(chunk * cut, (chunk + 1) * cut)
    far_cut = slice(HALF + chunk * cut, HALF + (chunk + 1) * cut)
    for block in range(4 * slots):
        span = slice((block % 4) * 128, (block % 4 + 1) * 128)
        pair = [half[block // 4] for half in halves]
        weight = jnp.concatenate([ref[span, near_cut] for ref in pair], axis=0)
        result = lax.dot_general(flat[:, :cut], weight, NT, preferred_element_type=jnp.float32)
        weight = jnp.concatenate([ref[span, far_cut] for ref in pair], axis=0)
        result = result + lax.dot_general(flat[:, cut:], weight, NT, preferred_element_type=jnp.float32)
        near = slice(block * 256, (block + 1) * 256)
        if chunk:
            result = result + acc_ref[:, near]
        if not last:
            out_ref[:, near] = result
            continue
        staged_ref[:, near] = result.astype(jnp.bfloat16)
        for core in range(2):
            shard = shard_of(*sizes, core, block)
            moves.append(
                pltpu.make_async_copy(
                    staged_ref.at[:, slice(block * 256 + core * 128, block * 256 + (core + 1) * 128)],
                    out_ref.at[:, columns(shard)],
                    out_sems.at[2 * block + core],
                )
            )
            moves[-1].start()
    for move in moves:
        move.wait()


def finish(sizes, chunk, parts, acc, halves, results):
    rows = parts[0].shape[0]
    slots = len(halves) // 2
    width = len(halves) * 512
    given = [inside(value) for value in list(parts) + ([acc] if chunk else []) + list(halves) + list(results)]
    out, specs = [pltpu.VMEM((rows, width), jnp.float32)], [VMEM]
    scratch = []
    if results:
        out += [pltpu.HBM((rows, width), jnp.bfloat16)] * 2
        specs += [HBM] * 2
        scratch = [pltpu.SemaphoreType.DMA((len(results),))]
    if chunk + 1 == CHUNKS:
        out[0], specs[0] = pltpu.HBM((rows, width), jnp.bfloat16), HBM
        scratch += [pltpu.VMEM((rows, width), jnp.bfloat16), pltpu.SemaphoreType.DMA((8 * slots,))]
    return pl.pallas_call(
        functools.partial(finish_kernel, sizes, chunk, len(parts), slots, len(results)),
        out_shape=out,
        in_specs=[VMEM] * len(given),
        out_specs=specs,
        scratch_shapes=scratch,
        compiler_params=params(16),
        cost_estimate=cost(2 * rows * width * 2 * HALF // CHUNKS, 10 << 20),
        name="finish",
    )(*given)


def halved(slot, depth):
    return slot == 0 or slot == depth - 1 or depth % 2 == 1


def shards(sizes, queries, layer_input, key_value_weight, output_gradient, document_lengths):
    depth, across = sizes
    inputs = layer_input[0]
    reach = across // 4

    queries, gradient = queries[0], output_gradient[0]

    def moved(value, target):
        pairs = []
        for a in range(depth):
            for b in range(across):
                to = target(a, b)
                if to is not None:
                    pairs.append((a * across + b, to[0] * across + to[1]))
        return lax.ppermute(value, AXES, pairs)

    def over_x(value):
        return moved(value, lambda a, b: (a, b ^ 2))

    def over_y(value):
        return moved(value, lambda a, b: (a, b ^ 4))

    def over_core(value):
        return moved(value, lambda a, b: (a, b ^ 1))

    def along(value, steps):
        return moved(value, lambda a, b: ((a + steps) % depth, b))

    def behind(value, steps):
        return moved(value, lambda a, b: (a, b + steps) if 0 <= b + steps < across else None)

    by_hand = across == 8 and key_value_weight.shape[0] == 128
    if by_hand:
        held = key_value_weight
        acc, mine, theirs = None, [], []
        other = over_core(inputs)
        queries, gradient = fetch(queries, gradient)
        lined = arrange(sizes, inputs, other)
        for slot in range(depth):
            after = along(held, 1) if slot + 1 < depth else None
            rx, ry = over_x(held), over_y(held)
            pieces = [held, rx, ry]
            if halved(slot, depth):
                pieces += [over_y(rx[:, :HALF]), over_x(ry[:, HALF:])]
            elif slot % 2:
                pieces += [over_y(rx)]
            else:
                pieces += [over_x(ry)]
            packed, acc = project(slot, lined, acc, pieces, slot + 1 == depth)
            mine.append(packed)
            theirs.append(over_core(packed))
            if slot + 1 < depth:
                acc = acc[0]
            held = after
        got = over_core(acc[1])
        chunks = join(acc[0], got)
    else:
        full = lax.all_gather(key_value_weight, AXES, axis=0, tiled=True)
        flat = jnp.dot(inputs, full, preferred_element_type=jnp.float32).astype(jnp.bfloat16)
        cut = CHUNK_HEADS * HEAD_SIZE
        chunks = [
            jnp.concatenate([flat[:, c * cut : (c + 1) * cut], flat[:, HALF + c * cut : HALF + (c + 1) * cut]], axis=1)
            for c in range(CHUNKS)
        ]
    kvs = [[chunk] + [behind(chunk, step) for step in range(1, reach + 1)] for chunk in chunks]
    results, parts = [], []
    for chunk in range(CHUNKS):
        made, pieces = attend(document_lengths, queries, gradient, kvs[chunk], chunk)
        results += made
        parts.append([pieces[0]] + [behind(pieces[step], -step) for step in range(1, reach + 1)])
    if by_hand:
        acc = None
        for chunk in range(CHUNKS):
            acc = finish(
                sizes, chunk, parts[chunk], acc and acc[0], mine + theirs, [] if chunk else results
            )
            if chunk == 0:
                attended, query_grad = acc[1:]
        input_grad = acc[0]
    else:
        sums = []
        for group in parts:
            total = group[0]
            for piece in group[1:]:
                total = total + piece.astype(jnp.float32)
            sums.append(total.astype(jnp.bfloat16))
        cut = CHUNK_HEADS * HEAD_SIZE
        flat = jnp.concatenate([s[:, :cut] for s in sums] + [s[:, cut:] for s in sums], axis=1)
        input_grad = lax.dot_general(flat, full, NT, preferred_element_type=jnp.float32).astype(jnp.bfloat16)
        attended = jnp.concatenate(results[0::2], axis=1)
        query_grad = jnp.concatenate(results[1::2], axis=1)
    return (attended[None], query_grad[None], input_grad[None])


def solution(mesh):
    sizes = (mesh.shape["dp"], mesh.shape["ctx"])
    return jax.shard_map(
        functools.partial(shards, sizes),
        mesh=mesh,
        in_specs=(
            P("dp", "ctx", None),
            P("dp", "ctx", None),
            P(("dp", "ctx"), None),
            P("dp", "ctx", None),
            P("dp", None),
        ),
        out_specs=(P("dp", "ctx", None), P("dp", "ctx", None), P("dp", "ctx", None)),
        check_vma=False,
    )
```

profile of v0, /device:TPU:5, one launch (start us, length us, event | category | flops | bytes accessed | tf_op | source)
XLA Modules:
  0.0 113.8 jit_solution(5898644465978323669)
XLA Ops:
  2.9 7.1 %collective-permute-done.5.refs_1_ = bf16[128,1024]{1,0:T(8,128)(2,1)S(1)} collective-permute-done((bf16[128,1024]{1,0:T(8,128)(2,1)}, bf16[128,1024]{1,0:T(8,128)(2,1)S(1)}, u32[]{:S(2)}, u32[]{:S(2)}) %collective-permute-start.5) | collective-permute-done | bytes 262176 | tf_op jit(solution)/shard_map/ppermute | solution.py:370
  11.4 6.8 %collective-permute-done.9.refs_1_ = bf16[128,1024]{1,0:T(8,128)(2,1)S(1)} collective-permute-done((bf16[128,1024]{1,0:T(8,128)(2,1)S(1)}, bf16[128,1024]{1,0:T(8,128)(2,1)S(1)}, u32[]{:S(2)}, u32[]{:S(2)}) %collective-permute-start.9) | collective-permute-done | bytes 262176 | tf_op jit(solution)/shard_map/ppermute | solution.py:370
  22.8 2.8 %collective-permute-done.13.refs_1_ = bf16[128,1024]{1,0:T(8,128)(2,1)S(1)} collective-permute-done((bf16[128,1024]{1,0:T(8,128)(2,1)S(1)}, bf16[128,1024]{1,0:T(8,128)(2,1)S(1)}, u32[]{:S(2)}, u32[]{:S(2)}) %collective-permute-start.13) | collective-permute-done | bytes 262176 | tf_op jit(solution)/shard_map/ppermute | solution.py:370
  29.7 3.8 %collective-permute-done.15.refs_3_ = bf16[128,1024]{1,0:T(8,128)(2,1)S(1)} collective-permute-done((bf16[128,1024]{1,0:T(8,128)(2,1)S(1)}, bf16[128,1024]{1,0:T(8,128)(2,1)S(1)}, u32[]{:S(2)}, u32[]{:S(2)}) %collective-permute-start.15) | collective-permute-done | bytes 262176 | tf_op jit(solution)/shard_map/ppermute | solution.py:370
  35.0 4.1 %collective-permute-done.7.refs_3_ = bf16[128,1024]{1,0:T(8,128)(2,1)S(1)} collective-permute-done((bf16[128,1024]{1,0:T(8,128)(2,1)S(1)}, bf16[128,1024]{1,0:T(8,128)(2,1)S(1)}, u32[]{:S(2)}, u32[]{:S(2)}) %collective-permute-start.7) | collective-permute-done | bytes 262176 | tf_op jit(solution)/shard_map/ppermute | solution.py:370
  42.2 2.6 %collective-permute-done.8.refs_4_ = bf16[128,1024]{1,0:T(8,128)(2,1)S(1)} collective-permute-done((bf16[128,1024]{1,0:T(8,128)(2,1)S(1)}, bf16[128,1024]{1,0:T(8,128)(2,1)S(1)}, u32[]{:S(2)}, u32[]{:S(2)}) %collective-permute-start.8) | collective-permute-done | bytes 262176 | tf_op jit(solution)/shard_map/ppermute | solution.py:370
  48.0 6.2 %collective-permute-start.18 = (f32[128,1024]{1,0:T(8,128)S(1)}, f32[128,1024]{1,0:T(8,128)S(1)}, u32[]{:S(2)}, u32[]{:S(2)}) collective-permute-start(f32[128,1024]{1,0:T(8,128)S(1)} %get-tuple-element.35), channel_id=1, source_target_pairs={{0,1},{1,0},{2,3},{3,2},{4,5},{5,4},{6,7},{7,6},{8,9},{9,8},{10,11... | collective-permute-start | bytes 1572872 | tf_op jit(solution)/shard_map/ppermute | solution.py:370
  55.9 2.3 %collective-permute-start.20 = (bf16[128,512]{1,0:T(8,128)(2,1)S(1)}, bf16[128,512]{1,0:T(8,128)(2,1)S(1)}, u32[]{:S(2)}, u32[]{:S(2)}) collective-permute-start(bf16[128,512]{1,0:T(8,128)(2,1)S(1)} %get-tuple-element.36.refs_0_), channel_id=1, source_target_pairs={{0,2},{1,3},{2,4},{3,5},{4,6},{5,7},{8,10},{9,11},{10,12},{11,13},... | collective-permute-start | bytes 393224 | tf_op jit(solution)/shard_map/ppermute | solution.py:370
  59.4 3.9 %collective-permute-done.20.refs_2_ = bf16[128,512]{1,0:T(8,128)(2,1)S(1)} collective-permute-done((bf16[128,512]{1,0:T(8,128)(2,1)S(1)}, bf16[128,512]{1,0:T(8,128)(2,1)S(1)}, u32[]{:S(2)}, u32[]{:S(2)}) %collective-permute-start.20) | collective-permute-done | bytes 131104 | tf_op jit(solution)/shard_map/ppermute | solution.py:370
  63.3 2.5 %collective-permute-start.19 = (bf16[128,512]{1,0:T(8,128)(2,1)S(1)}, bf16[128,512]{1,0:T(8,128)(2,1)S(1)}, u32[]{:S(2)}, u32[]{:S(2)}) collective-permute-start(bf16[128,512]{1,0:T(8,128)(2,1)S(1)} %get-tuple-element.36.refs_0_), channel_id=1, source_target_pairs={{0,1},{1,2},{2,3},{3,4},{4,5},{5,6},{6,7},{8,9},{9,10},{10,11},{11... | collective-permute-start | bytes 393224 | tf_op jit(solution)/shard_map/ppermute | solution.py:370
  65.9 1.9 %collective-permute-done.19.refs_1_ = bf16[128,512]{1,0:T(8,128)(2,1)S(1)} collective-permute-done((bf16[128,512]{1,0:T(8,128)(2,1)S(1)}, bf16[128,512]{1,0:T(8,128)(2,1)S(1)}, u32[]{:S(2)}, u32[]{:S(2)}) %collective-permute-start.19) | collective-permute-done | bytes 131104 | tf_op jit(solution)/shard_map/ppermute | solution.py:370
  67.8 1.9 %collective-permute-start.28 = (bf16[128,512]{1,0:T(8,128)(2,1)S(1)}, bf16[128,512]{1,0:T(8,128)(2,1)S(1)}, u32[]{:S(2)}, u32[]{:S(2)}) collective-permute-start(bf16[128,512]{1,0:T(8,128)(2,1)S(1)} %get-tuple-element.46.refs_0_), channel_id=1, source_target_pairs={{0,2},{1,3},{2,4},{3,5},{4,6},{5,7},{8,10},{9,11},{10,12},{11,13},... | collective-permute-start | bytes 393224 | tf_op jit(solution)/shard_map/ppermute | solution.py:370
  71.3 3.6 %collective-permute-done.28.refs_2_ = bf16[128,512]{1,0:T(8,128)(2,1)S(1)} collective-permute-done((bf16[128,512]{1,0:T(8,128)(2,1)S(1)}, bf16[128,512]{1,0:T(8,128)(2,1)S(1)}, u32[]{:S(2)}, u32[]{:S(2)}) %collective-permute-start.28) | collective-permute-done | bytes 131104 | tf_op jit(solution)/shard_map/ppermute | solution.py:370
  74.9 5.2 %collective-permute-start.27 = (bf16[128,512]{1,0:T(8,128)(2,1)S(1)}, bf16[128,512]{1,0:T(8,128)(2,1)S(1)}, u32[]{:S(2)}, u32[]{:S(2)}) collective-permute-start(bf16[128,512]{1,0:T(8,128)(2,1)S(1)} %get-tuple-element.46.refs_0_), channel_id=1, source_target_pairs={{0,1},{1,2},{2,3},{3,4},{4,5},{5,6},{6,7},{8,9},{9,10},{10,11},{11... | collective-permute-start | bytes 393224 | tf_op jit(solution)/shard_map/ppermute | solution.py:370
  80.1 4.8 %attend.2 = (bf16[128,2048]{1,0:T(8,128)(2,1)S(1)}, bf16[128,2048]{1,0:T(8,128)(2,1)S(1)}, f32[128,512]{1,0:T(8,128)S(1)}, bf16[128,512]{1,0:T(8,128)(2,1)S(1)}, bf16[128,512]{1,0:T(8,128)(2,1)S(1)}) custom-call(s32[1,8]{1,0:T(1,128)S(1)} %copy-done.2, bf16[128,4096]{1,0:T(8,128)(2,1)S(1)} %get-tuple-element.29.q_ref, ...), custom_call_target="tpu_custom_call" | custom-call | flops 2415919104 | bytes 4194304 | tf_op jit(solution)/shard_map/attend/pallas_call | solution.py:251
  85.0 3.6 %collective-permute-start.21 = (bf16[128,512]{1,0:T(8,128)(2,1)S(1)}, bf16[128,512]{1,0:T(8,128)(2,1)S(1)}, u32[]{:S(2)}, u32[]{:S(2)}) collective-permute-start(bf16[128,512]{1,0:T(8,128)(2,1)S(1)} %get-tuple-element.38), channel_id=1, source_target_pairs={{1,0},{2,1},{3,2},{4,3},{5,4},{6,5},{7,6},{9,8},{10,9},{11,10},{12... | collective-permute-start | bytes 393224 | tf_op jit(solution)/shard_map/ppermute | solution.py:370
  88.6 2.7 %collective-permute-done.21.refs_1_ = bf16[128,512]{1,0:T(8,128)(2,1)S(1)} collective-permute-done((bf16[128,512]{1,0:T(8,128)(2,1)S(1)}, bf16[128,512]{1,0:T(8,128)(2,1)S(1)}, u32[]{:S(2)}, u32[]{:S(2)}) %collective-permute-start.21) | collective-permute-done | bytes 131104 | tf_op jit(solution)/shard_map/ppermute | solution.py:370
  91.3 6.5 %collective-permute-start.22 = (bf16[128,512]{1,0:T(8,128)(2,1)S(1)}, bf16[128,512]{1,0:T(8,128)(2,1)S(1)}, u32[]{:S(2)}, u32[]{:S(2)}) collective-permute-start(bf16[128,512]{1,0:T(8,128)(2,1)S(1)} %get-tuple-element.39), channel_id=1, source_target_pairs={{2,0},{3,1},{4,2},{5,3},{6,4},{7,5},{10,8},{11,9},{12,10},{13,11},... | collective-permute-start | bytes 393224 | tf_op jit(solution)/shard_map/ppermute | solution.py:370
  97.8 4.8 %attend.3 = (bf16[128,2048]{1,0:T(8,128)(2,1)S(1)}, bf16[128,2048]{1,0:T(8,128)(2,1)S(1)}, f32[128,512]{1,0:T(8,128)S(1)}, bf16[128,512]{1,0:T(8,128)(2,1)S(1)}, bf16[128,512]{1,0:T(8,128)(2,1)S(1)}) custom-call(s32[1,8]{1,0:T(1,128)S(1)} %copy-done.2, bf16[128,4096]{1,0:T(8,128)(2,1)S(1)} %get-tuple-element.29.q_ref, ...), custom_call_target="tpu_custom_call" | custom-call | flops 2415919104 | bytes 4194304 | tf_op jit(solution)/shard_map/attend/pallas_call | solution.py:251
  102.6 1.9 %collective-permute-start.29 = (bf16[128,512]{1,0:T(8,128)(2,1)S(1)}, bf16[128,512]{1,0:T(8,128)(2,1)S(1)}, u32[]{:S(2)}, u32[]{:S(2)}) collective-permute-start(bf16[128,512]{1,0:T(8,128)(2,1)S(1)} %get-tuple-element.52), channel_id=1, source_target_pairs={{1,0},{2,1},{3,2},{4,3},{5,4},{6,5},{7,6},{9,8},{10,9},{11,10},{12... | collective-permute-start | bytes 393224 | tf_op jit(solution)/shard_map/ppermute | solution.py:370
  104.6 1.9 %collective-permute-start.30 = (bf16[128,512]{1,0:T(8,128)(2,1)S(1)}, bf16[128,512]{1,0:T(8,128)(2,1)S(1)}, u32[]{:S(2)}, u32[]{:S(2)}) collective-permute-start(bf16[128,512]{1,0:T(8,128)(2,1)S(1)} %get-tuple-element.53), channel_id=1, source_target_pairs={{2,0},{3,1},{4,2},{5,3},{6,4},{7,5},{10,8},{11,9},{12,10},{13,11},... | collective-permute-start | bytes 393224 | tf_op jit(solution)/shard_map/ppermute | solution.py:370
  106.5 2.7 %finish.2 = (f32[128,4096]{1,0:T(8,128)S(1)}, bf16[128,4096]{1,0:T(8,128)(2,1)}, bf16[128,4096]{1,0:T(8,128)(2,1)}) custom-call(f32[128,512]{1,0:T(8,128)S(1)} %get-tuple-element.37.refs_0_, bf16[128,512]{1,0:T(8,128)(2,1)S(1)} %collective-permute-done.21.refs_1_, bf16[128,512]{1,0:T(8,128)(2,1)S(1)} %collective-permute-done.22.refs_2_, ...), custom_call_target="tpu_custom_call" | custom-call | flops 536870912 | bytes 10485760 | tf_op jit(solution)/shard_map/finish/pallas_call | solution.py:340
  109.2 2.0 %collective-permute-done.30.refs_2_ = bf16[128,512]{1,0:T(8,128)(2,1)S(1)} collective-permute-done((bf16[128,512]{1,0:T(8,128)(2,1)S(1)}, bf16[128,512]{1,0:T(8,128)(2,1)S(1)}, u32[]{:S(2)}, u32[]{:S(2)}) %collective-permute-start.30) | collective-permute-done | bytes 131104 | tf_op jit(solution)/shard_map/ppermute | solution.py:370
  111.2 2.5 %finish.3 = bf16[128,4096]{1,0:T(8,128)(2,1)} custom-call(f32[128,512]{1,0:T(8,128)S(1)} %get-tuple-element.51.refs_0_, bf16[128,512]{1,0:T(8,128)(2,1)S(1)} %collective-permute-done.29.refs_1_, bf16[128,512]{1,0:T(8,128)(2,1)S(1)} %collective-permute-done.30.refs_2_, f32[128,4096]{1,0:T(8,128)S(1)} %get-tuple-element.54.refs_3_, ...), custom_call_target="tpu_custom_call" | custom-call | flops 536870912 | bytes 10485760 | tf_op jit(solution)/shard_map/finish/pallas_call | solution.py:340
  (59 shorter events, 24.6 us)
Async XLA Ops:
  0.6 9.4 %collective-permute-start.5 = (bf16[128,1024]{1,0:T(8,128)(2,1)}, bf16[128,1024]{1,0:T(8,128)(2,1)S(1)}, u32[]{:S(2)}, u32[]{:S(2)}) collective-permute-start(bf16[128,1024]{1,0:T(8,128)(2,1)} %refs_0_.1), channel_id=1, source_target_pairs={{0,8},{1,9},{2,10},{3,11},{4,12},{5,13},{6,14},{7,15},{8,16},{9,17... | collective-permute-start | bytes 786440 | tf_op jit(solution)/shard_map/ppermute | solution.py:370
  2.0 37.5 %collective-permute-start = (bf16[128,4096]{1,0:T(8,128)(2,1)}, bf16[128,4096]{1,0:T(8,128)(2,1)S(1)}, u32[]{:S(2)}, u32[]{:S(2)}) collective-permute-start(bf16[128,4096]{1,0:T(8,128)(2,1)} %bitcast.6), channel_id=1, source_target_pairs={{0,1},{1,0},{2,3},{3,2},{4,5},{5,4},{6,7},{7,6},{8,9},{9,8},{10,11... | collective-permute-start | bytes 3145736 | tf_op jit(solution)/shard_map/ppermute | solution.py:370
  10.0 8.2 %collective-permute-start.9 = (bf16[128,1024]{1,0:T(8,128)(2,1)S(1)}, bf16[128,1024]{1,0:T(8,128)(2,1)S(1)}, u32[]{:S(2)}, u32[]{:S(2)}) collective-permute-start(bf16[128,1024]{1,0:T(8,128)(2,1)S(1)} %collective-permute-done.5.refs_1_), channel_id=1, source_target_pairs={{0,8},{1,9},{2,10},{3,11},{4,12},{5,13},{6,14},{7,15},{8,16},{9,17... | collective-permute-start | bytes 786440 | tf_op jit(solution)/shard_map/ppermute | solution.py:370
  10.0 8.2 %collective-permute-start.2 = (bf16[128,1024]{1,0:T(8,128)(2,1)}, bf16[128,1024]{1,0:T(8,128)(2,1)S(1)}, u32[]{:S(2)}, u32[]{:S(2)}) collective-permute-start(bf16[128,1024]{1,0:T(8,128)(2,1)} %refs_0_.1), channel_id=1, source_target_pairs={{0,4},{1,5},{2,6},{3,7},{4,0},{5,1},{6,2},{7,3},{8,12},{9,13},{10,... | collective-permute-start | bytes 786440 | tf_op jit(solution)/shard_map/ppermute | solution.py:370
  10.5 9.0 %collective-permute-start.1 = (bf16[128,1024]{1,0:T(8,128)(2,1)}, bf16[128,1024]{1,0:T(8,128)(2,1)S(1)}, u32[]{:S(2)}, u32[]{:S(2)}) collective-permute-start(bf16[128,1024]{1,0:T(8,128)(2,1)} %refs_0_.1), channel_id=1, source_target_pairs={{0,2},{1,3},{2,0},{3,1},{4,6},{5,7},{6,4},{7,5},{8,10},{9,11},{10,... | collective-permute-start | bytes 786440 | tf_op jit(solution)/shard_map/ppermute | solution.py:370
  18.2 7.3 %collective-permute-start.13 = (bf16[128,1024]{1,0:T(8,128)(2,1)S(1)}, bf16[128,1024]{1,0:T(8,128)(2,1)S(1)}, u32[]{:S(2)}, u32[]{:S(2)}) collective-permute-start(bf16[128,1024]{1,0:T(8,128)(2,1)S(1)} %collective-permute-done.9.refs_1_), channel_id=1, source_target_pairs={{0,8},{1,9},{2,10},{3,11},{4,12},{5,13},{6,14},{7,15},{8,16},{9,17... | collective-permute-start | bytes 786440 | tf_op jit(solution)/shard_map/ppermute | solution.py:370
  19.8 7.2 %collective-permute-start.6 = (bf16[128,1024]{1,0:T(8,128)(2,1)S(1)}, bf16[128,1024]{1,0:T(8,128)(2,1)S(1)}, u32[]{:S(2)}, u32[]{:S(2)}) collective-permute-start(bf16[128,1024]{1,0:T(8,128)(2,1)S(1)} %collective-permute-done.5.refs_1_), channel_id=1, source_target_pairs={{0,2},{1,3},{2,0},{3,1},{4,6},{5,7},{6,4},{7,5},{8,10},{9,11},{10,... | collective-permute-start | bytes 786440 | tf_op jit(solution)/shard_map/ppermute | solution.py:370
  22.1 6.9 %collective-permute-start.11 = (bf16[128,1024]{1,0:T(8,128)(2,1)S(1)}, bf16[128,1024]{1,0:T(8,128)(2,1)S(1)}, u32[]{:S(2)}, u32[]{:S(2)}) collective-permute-start(bf16[128,1024]{1,0:T(8,128)(2,1)S(1)} %collective-permute-done.9.refs_1_), channel_id=1, source_target_pairs={{0,4},{1,5},{2,6},{3,7},{4,0},{5,1},{6,2},{7,3},{8,12},{9,13},{10,... | collective-permute-start | bytes 786440 | tf_op jit(solution)/shard_map/ppermute | solution.py:370
  25.5 8.0 %collective-permute-start.15 = (bf16[128,1024]{1,0:T(8,128)(2,1)S(1)}, bf16[128,1024]{1,0:T(8,128)(2,1)S(1)}, u32[]{:S(2)}, u32[]{:S(2)}) collective-permute-start(bf16[128,1024]{1,0:T(8,128)(2,1)S(1)} %collective-permute-done.13.refs_1_), channel_id=1, source_target_pairs={{0,4},{1,5},{2,6},{3,7},{4,0},{5,1},{6,2},{7,3},{8,12},{9,13},{10,... | collective-permute-start | bytes 786440 | tf_op jit(solution)/shard_map/ppermute | solution.py:370
  26.4 7.5 %collective-permute-start.14 = (bf16[128,1024]{1,0:T(8,128)(2,1)S(1)}, bf16[128,1024]{1,0:T(8,128)(2,1)S(1)}, u32[]{:S(2)}, u32[]{:S(2)}) collective-permute-start(bf16[128,1024]{1,0:T(8,128)(2,1)S(1)} %collective-permute-done.13.refs_1_), channel_id=1, source_target_pairs={{0,2},{1,3},{2,0},{3,1},{4,6},{5,7},{6,4},{7,5},{8,10},{9,11},{10,... | collective-permute-start | bytes 786440 | tf_op jit(solution)/shard_map/ppermute | solution.py:370
  27.0 12.2 %collective-permute-start.7 = (bf16[128,1024]{1,0:T(8,128)(2,1)S(1)}, bf16[128,1024]{1,0:T(8,128)(2,1)S(1)}, u32[]{:S(2)}, u32[]{:S(2)}) collective-permute-start(bf16[128,1024]{1,0:T(8,128)(2,1)S(1)} %collective-permute-done.5.refs_1_), channel_id=1, source_target_pairs={{0,4},{1,5},{2,6},{3,7},{4,0},{5,1},{6,2},{7,3},{8,12},{9,13},{10,... | collective-permute-start | bytes 786440 | tf_op jit(solution)/shard_map/ppermute | solution.py:370
  29.0 15.7 %collective-permute-start.8 = (bf16[128,1024]{1,0:T(8,128)(2,1)S(1)}, bf16[128,1024]{1,0:T(8,128)(2,1)S(1)}, u32[]{:S(2)}, u32[]{:S(2)}) collective-permute-start(bf16[128,1024]{1,0:T(8,128)(2,1)S(1)} %collective-permute-done.6.refs_2_), channel_id=1, source_target_pairs={{0,4},{1,5},{2,6},{3,7},{4,0},{5,1},{6,2},{7,3},{8,12},{9,13},{10,... | collective-permute-start | bytes 786440 | tf_op jit(solution)/shard_map/ppermute | solution.py:370
  33.5 11.7 %collective-permute-start.10 = (bf16[128,1024]{1,0:T(8,128)(2,1)S(1)}, bf16[128,1024]{1,0:T(8,128)(2,1)S(1)}, u32[]{:S(2)}, u32[]{:S(2)}) collective-permute-start(bf16[128,1024]{1,0:T(8,128)(2,1)S(1)} %collective-permute-done.9.refs_1_), channel_id=1, source_target_pairs={{0,2},{1,3},{2,0},{3,1},{4,6},{5,7},{6,4},{7,5},{8,10},{9,11},{10,... | collective-permute-start | bytes 786440 | tf_op jit(solution)/shard_map/ppermute | solution.py:370
  33.9 11.3 %collective-permute-start.12 = (bf16[128,1024]{1,0:T(8,128)(2,1)S(1)}, bf16[128,1024]{1,0:T(8,128)(2,1)S(1)}, u32[]{:S(2)}, u32[]{:S(2)}) collective-permute-start(bf16[128,1024]{1,0:T(8,128)(2,1)S(1)} %collective-permute-done.11.refs_3_), channel_id=1, source_target_pairs={{0,2},{1,3},{2,0},{3,1},{4,6},{5,7},{6,4},{7,5},{8,10},{9,11},{10,... | collective-permute-start | bytes 786440 | tf_op jit(solution)/shard_map/ppermute | solution.py:370
  39.5 8.0 %collective-permute-start.16 = (bf16[128,512]{1,0:T(8,128)(2,1)S(1)}, bf16[128,512]{1,0:T(8,128)(2,1)S(1)}, u32[]{:S(2)}, u32[]{:S(2)}) collective-permute-start(bf16[128,512]{1,0:T(8,128)(2,1)S(1)} %slice.18), channel_id=1, source_target_pairs={{0,4},{1,5},{2,6},{3,7},{4,0},{5,1},{6,2},{7,3},{8,12},{9,13},{10,... | collective-permute-start | bytes 393224 | tf_op jit(solution)/shard_map/ppermute | solution.py:370
  48.0 7.8 %collective-permute-start.18 = (f32[128,1024]{1,0:T(8,128)S(1)}, f32[128,1024]{1,0:T(8,128)S(1)}, u32[]{:S(2)}, u32[]{:S(2)}) collective-permute-start(f32[128,1024]{1,0:T(8,128)S(1)} %get-tuple-element.35), channel_id=1, source_target_pairs={{0,1},{1,0},{2,3},{3,2},{4,5},{5,4},{6,7},{7,6},{8,9},{9,8},{10,11... | collective-permute-start | bytes 1572872 | tf_op jit(solution)/shard_map/ppermute | solution.py:370
  54.3 50.3 %collective-permute-start.25 = (bf16[512,1024]{1,0:T(8,128)(2,1)S(1)}, bf16[512,1024]{1,0:T(8,128)(2,1)S(1)}, u32[]{:S(2)}, u32[]{:S(2)}) collective-permute-start(bf16[512,1024]{1,0:T(8,128)(2,1)S(1)} %get-tuple-element.42.refs_5_.refs_6_), channel_id=1, source_target_pairs={{0,1},{1,0},{2,3},{3,2},{4,5},{5,4},{6,7},{7,6},{8,9},{9,8},{10,11... | collective-permute-start | bytes 3145736 | tf_op jit(solution)/shard_map/ppermute | solution.py:370
  55.9 7.5 %collective-permute-start.20 = (bf16[128,512]{1,0:T(8,128)(2,1)S(1)}, bf16[128,512]{1,0:T(8,128)(2,1)S(1)}, u32[]{:S(2)}, u32[]{:S(2)}) collective-permute-start(bf16[128,512]{1,0:T(8,128)(2,1)S(1)} %get-tuple-element.36.refs_0_), channel_id=1, source_target_pairs={{0,2},{1,3},{2,4},{3,5},{4,6},{5,7},{8,10},{9,11},{10,12},{11,13},... | collective-permute-start | bytes 393224 | tf_op jit(solution)/shard_map/ppermute | solution.py:370
  58.2 48.3 %collective-permute-start.24 = (bf16[512,1024]{1,0:T(8,128)(2,1)S(1)}, bf16[512,1024]{1,0:T(8,128)(2,1)S(1)}, u32[]{:S(2)}, u32[]{:S(2)}) collective-permute-start(bf16[512,1024]{1,0:T(8,128)(2,1)S(1)} %get-tuple-element.41.refs_4_.refs_5_), channel_id=1, source_target_pairs={{0,1},{1,0},{2,3},{3,2},{4,5},{5,4},{6,7},{7,6},{8,9},{9,8},{10,11... | collective-permute-start | bytes 3145736 | tf_op jit(solution)/shard_map/ppermute | solution.py:370
  58.9 47.6 %collective-permute-start.23 = (bf16[512,1024]{1,0:T(8,128)(2,1)S(1)}, bf16[512,1024]{1,0:T(8,128)(2,1)S(1)}, u32[]{:S(2)}, u32[]{:S(2)}) collective-permute-start(bf16[512,1024]{1,0:T(8,128)(2,1)S(1)} %get-tuple-element.40.refs_3_.refs_4_), channel_id=1, source_target_pairs={{0,1},{1,0},{2,3},{3,2},{4,5},{5,4},{6,7},{7,6},{8,9},{9,8},{10,11... | collective-permute-start | bytes 3145736 | tf_op jit(solution)/shard_map/ppermute | solution.py:370
  59.0 47.6 %collective-permute-start.26 = (bf16[512,1024]{1,0:T(8,128)(2,1)S(1)}, bf16[512,1024]{1,0:T(8,128)(2,1)S(1)}, u32[]{:S(2)}, u32[]{:S(2)}) collective-permute-start(bf16[512,1024]{1,0:T(8,128)(2,1)S(1)} %get-tuple-element.43.refs_6_.refs_7_), channel_id=1, source_target_pairs={{0,1},{1,0},{2,3},{3,2},{4,5},{5,4},{6,7},{7,6},{8,9},{9,8},{10,11... | collective-permute-start | bytes 3145736 | tf_op jit(solution)/shard_map/ppermute | solution.py:370
  67.8 7.1 %collective-permute-start.28 = (bf16[128,512]{1,0:T(8,128)(2,1)S(1)}, bf16[128,512]{1,0:T(8,128)(2,1)S(1)}, u32[]{:S(2)}, u32[]{:S(2)}) collective-permute-start(bf16[128,512]{1,0:T(8,128)(2,1)S(1)} %get-tuple-element.46.refs_0_), channel_id=1, source_target_pairs={{0,2},{1,3},{2,4},{3,5},{4,6},{5,7},{8,10},{9,11},{10,12},{11,13},... | collective-permute-start | bytes 393224 | tf_op jit(solution)/shard_map/ppermute | solution.py:370
  74.9 10.1 %collective-permute-start.27 = (bf16[128,512]{1,0:T(8,128)(2,1)S(1)}, bf16[128,512]{1,0:T(8,128)(2,1)S(1)}, u32[]{:S(2)}, u32[]{:S(2)}) collective-permute-start(bf16[128,512]{1,0:T(8,128)(2,1)S(1)} %get-tuple-element.46.refs_0_), channel_id=1, source_target_pairs={{0,1},{1,2},{2,3},{3,4},{4,5},{5,6},{6,7},{8,9},{9,10},{10,11},{11... | collective-permute-start | bytes 393224 | tf_op jit(solution)/shard_map/ppermute | solution.py:370
  91.3 11.3 %collective-permute-start.22 = (bf16[128,512]{1,0:T(8,128)(2,1)S(1)}, bf16[128,512]{1,0:T(8,128)(2,1)S(1)}, u32[]{:S(2)}, u32[]{:S(2)}) collective-permute-start(bf16[128,512]{1,0:T(8,128)(2,1)S(1)} %get-tuple-element.39), channel_id=1, source_target_pairs={{2,0},{3,1},{4,2},{5,3},{6,4},{7,5},{10,8},{11,9},{12,10},{13,11},... | collective-permute-start | bytes 393224 | tf_op jit(solution)/shard_map/ppermute | solution.py:370
  (10 other events, 114.3 us)
where the time goes:
time: 115 us; the launch traced here: 114 us
  starting transfers between devices  46.5 us (40%)
  waiting for transfers between devices  46.4 us (40%)
  Pallas kernels  18.5 us (16%)
  local copies, waits for them, and re-layouts  1.27 us (1%)
    ppermute x31, starting transfers between devices, moved(): return lax.ppermute(value, AXES, pairs)  46.5 us
    ppermute x31, waiting for transfers between devices, moved(): return lax.ppermute(value, AXES, pairs)  46.4 us
    pallas_call x2, Pallas kernels, attend(): pl.pallas_call(functools.partial(attend_kernel, chunk, reach), out_shape=...  9.67 us
    pallas_call x2, Pallas kernels, finish(): pl.pallas_call(functools.partial(finish_kernel, sizes, chunk, len(parts),...  5.14 us
  transfers between devices with their start and end apart: 31, of which 15 were waited for; matrix products, arithmetic and copies ran while one was open for 0% of the time, Pallas kernels for 14%

commit v1 on v0

--- a/solution.py
+++ b/solution.py
@@ -251,7 +251,7 @@
     outs = pl.pallas_call(
         functools.partial(attend_kernel, chunk, reach),
         out_shape=[whole, whole]
-        + [pltpu.VMEM(piece, jnp.float32 if j == 0 else jnp.bfloat16) for j in range(reach + 1)],
+        + [pltpu.VMEM(piece, jnp.float32 if j % 2 == 0 else jnp.bfloat16) for j in range(reach + 1)],
         in_specs=[SMEM] + [VMEM] * (reach + 3),
         out_specs=[VMEM] * (reach + 3),
         scratch_shapes=[
@@ -267,6 +267,25 @@
         name="attend",
     )(*given)
     return outs[:2], outs[2:]
+
+
+def combine_kernel(near_ref, swapped_ref, far_ref, here_ref, onward_ref):
+    second = lax.axis_index("ctx") % 2 == 1
+    swapped = swapped_ref[...].astype(jnp.float32)
+    here_ref[...] = near_ref[...] + jnp.where(second, 0.0, swapped)
+    onward_ref[...] = (far_ref[...].astype(jnp.float32) + jnp.where(second, swapped, 0.0)).astype(jnp.bfloat16)
+
+
+def combine(near, swapped, far):
+    return pl.pallas_call(
+        combine_kernel,
+        out_shape=[pltpu.VMEM(near.shape, jnp.float32), pltpu.VMEM(near.shape, jnp.bfloat16)],
+        in_specs=[VMEM] * 3,
+        out_specs=[VMEM] * 2,
+        compiler_params=params(16),
+        cost_estimate=cost(1 << 18, 1 << 20),
+        name="combine",
+    )(inside(near), inside(swapped), inside(far))
 
 
 def finish_kernel(sizes, chunk, terms, slots, extra, *refs):
@@ -349,10 +368,6 @@
     )(*given)
 
 
-def halved(slot, depth):
-    return slot == 0 or slot == depth - 1 or depth % 2 == 1
-
-
 def shards(sizes, queries, layer_input, key_value_weight, output_gradient, document_lengths):
     depth, across = sizes
     inputs = layer_input[0]
@@ -384,29 +399,33 @@
     def behind(value, steps):
         return moved(value, lambda a, b: (a, b + steps) if 0 <= b + steps < across else None)
 
-    by_hand = across == 8 and key_value_weight.shape[0] == 128
+    by_hand = across == 8 and depth > 2 and key_value_weight.shape[0] == 128
     if by_hand:
-        held = key_value_weight
-        acc, mine, theirs = None, [], []
+        own, last = key_value_weight, depth - 1
+        held, acc, mine, theirs = own, None, [], []
         other = over_core(inputs)
         queries, gradient = fetch(queries, gradient)
         lined = arrange(sizes, inputs, other)
         for slot in range(depth):
-            after = along(held, 1) if slot + 1 < depth else None
-            rx, ry = over_x(held), over_y(held)
+            held = along(held, 1) if slot else own
+            if slot == last:
+                rx, ry = along(side_x, slot), along(side_y, slot)
+            else:
+                rx, ry = over_x(held), over_y(held)
+            if slot == 0:
+                side_x, side_y = rx, ry
             pieces = [held, rx, ry]
-            if halved(slot, depth):
+            if slot == last:
+                pieces += [over_y(rx)]
+            elif slot == last - 1:
+                pieces += [over_x(ry)]
+            else:
                 pieces += [over_y(rx[:, :HALF]), over_x(ry[:, HALF:])]
-            elif slot % 2:
-                pieces += [over_y(rx)]
-            else:
-                pieces += [over_x(ry)]
             packed, acc = project(slot, lined, acc, pieces, slot + 1 == depth)
             mine.append(packed)
             theirs.append(over_core(packed))
             if slot + 1 < depth:
                 acc = acc[0]
-            held = after
         got = over_core(acc[1])
         chunks = join(acc[0], got)
     else:
@@ -422,7 +441,12 @@
     for chunk in range(CHUNKS):
         made, pieces = attend(document_lengths, queries, gradient, kvs[chunk], chunk)
         results += made
-        parts.append([pieces[0]] + [behind(pieces[step], -step) for step in range(1, reach + 1)])
+        if by_hand:
+            swapped = over_core(pieces[1])
+            here, onward = combine(pieces[0], swapped, pieces[2])
+            parts.append([here, behind(onward, -2)])
+        else:
+            parts.append([pieces[0]] + [behind(pieces[step], -step) for step in range(1, reach + 1)])
     if by_hand:
         acc = None
         for chunk in range(CHUNKS):

time: 115 us -> 102 us (0.89)
  the two profiles are of different devices: /device:TPU:5 before, /device:TPU:0 now
where the time goes in v1:
time: 102 us; the launch traced here: 101 us
  starting transfers between devices  42.6 us (42%)
  waiting for transfers between devices  37.7 us (37%)
  Pallas kernels  18.7 us (18%)
  local copies, waits for them, and re-layouts  1.27 us (1%)
  between operations  1.08 us (1%)
    ppermute x31, starting transfers between devices, moved(): return lax.ppermute(value, AXES, pairs)  42.6 us
    ppermute x31, waiting for transfers between devices, moved(): return lax.ppermute(value, AXES, pairs)  37.7 us
    pallas_call x2, Pallas kernels, attend(): pl.pallas_call(functools.partial(attend_kernel, chunk, reach), out_shape=...  9.68 us
    pallas_call x2, Pallas kernels, finish(): pl.pallas_call(functools.partial(finish_kernel, sizes, chunk, len(parts),...  5.15 us
  transfers between devices with their start and end apart: 31, of which 14 were waited for; matrix products, arithmetic and copies ran while one was open for 0% of the time, Pallas kernels for 15%

profile of v1, /device:TPU:0, one launch (start us, length us, event | category | flops | bytes accessed | tf_op | source)
XLA Modules:
  0.0 101.4 jit_solution(17825881820112993627)
XLA Ops:
  1.2 2.6 %collective-permute-start.5 = (bf16[128,1024]{1,0:T(8,128)(2,1)}, bf16[128,1024]{1,0:T(8,128)(2,1)S(1)}, u32[]{:S(2)}, u32[]{:S(2)}) collective-permute-start(bf16[128,1024]{1,0:T(8,128)(2,1)} %refs_0_.1), channel_id=1, source_target_pairs={{0,8},{1,9},{2,10},{3,11},{4,12},{5,13},{6,14},{7,15},{8,16},{9,17... | collective-permute-start | bytes 786440 | tf_op jit(solution)/shard_map/ppermute | solution.py:385
  6.8 6.1 %collective-permute-done.5.refs_1_ = bf16[128,1024]{1,0:T(8,128)(2,1)S(1)} collective-permute-done((bf16[128,1024]{1,0:T(8,128)(2,1)}, bf16[128,1024]{1,0:T(8,128)(2,1)S(1)}, u32[]{:S(2)}, u32[]{:S(2)}) %collective-permute-start.5) | collective-permute-done | bytes 262176 | tf_op jit(solution)/shard_map/ppermute | solution.py:385
  13.0 1.5 %collective-permute-start.7 = (bf16[128,1024]{1,0:T(8,128)(2,1)S(1)}, bf16[128,1024]{1,0:T(8,128)(2,1)S(1)}, u32[]{:S(2)}, u32[]{:S(2)}) collective-permute-start(bf16[128,1024]{1,0:T(8,128)(2,1)S(1)} %collective-permute-done.5.refs_1_), channel_id=1, source_target_pairs={{0,4},{1,5},{2,6},{3,7},{4,0},{5,1},{6,2},{7,3},{8,12},{9,13},{10,... | collective-permute-start | bytes 786440 | tf_op jit(solution)/shard_map/ppermute | solution.py:385
  16.0 3.8 %collective-permute-start.15 = (bf16[128,1024]{1,0:T(8,128)(2,1)S(1)}, bf16[128,1024]{1,0:T(8,128)(2,1)S(1)}, u32[]{:S(2)}, u32[]{:S(2)}) collective-permute-start(bf16[128,1024]{1,0:T(8,128)(2,1)S(1)} %collective-permute-done.1.refs_1_), channel_id=1, source_target_pairs={{0,24},{1,25},{2,26},{3,27},{4,28},{5,29},{6,30},{7,31},{8,0},{9,1... | collective-permute-start | bytes 786440 | tf_op jit(solution)/shard_map/ppermute | solution.py:385
  19.8 4.2 %collective-permute-done.10.refs_1_ = bf16[128,1024]{1,0:T(8,128)(2,1)S(1)} collective-permute-done((bf16[128,1024]{1,0:T(8,128)(2,1)S(1)}, bf16[128,1024]{1,0:T(8,128)(2,1)S(1)}, u32[]{:S(2)}, u32[]{:S(2)}) %collective-permute-start.10) | collective-permute-done | bytes 262176 | tf_op jit(solution)/shard_map/ppermute | solution.py:385
  24.0 1.5 %collective-permute-start.12 = (bf16[128,1024]{1,0:T(8,128)(2,1)S(1)}, bf16[128,1024]{1,0:T(8,128)(2,1)S(1)}, u32[]{:S(2)}, u32[]{:S(2)}) collective-permute-start(bf16[128,1024]{1,0:T(8,128)(2,1)S(1)} %collective-permute-done.10.refs_1_), channel_id=1, source_target_pairs={{0,4},{1,5},{2,6},{3,7},{4,0},{5,1},{6,2},{7,3},{8,12},{9,13},{10,... | collective-permute-start | bytes 786440 | tf_op jit(solution)/shard_map/ppermute | solution.py:385
  27.7 4.0 %collective-permute-done.4.refs_4_ = bf16[128,512]{1,0:T(8,128)(2,1)S(1)} collective-permute-done((bf16[128,512]{1,0:T(8,128)(2,1)S(1)}, bf16[128,512]{1,0:T(8,128)(2,1)S(1)}, u32[]{:S(2)}, u32[]{:S(2)}) %collective-permute-start.4) | collective-permute-done | bytes 131104 | tf_op jit(solution)/shard_map/ppermute | solution.py:385
  33.3 1.5 %collective-permute-start.8 = (bf16[128,512]{1,0:T(8,128)(2,1)S(1)}, bf16[128,512]{1,0:T(8,128)(2,1)S(1)}, u32[]{:S(2)}, u32[]{:S(2)}) collective-permute-start(bf16[128,512]{1,0:T(8,128)(2,1)S(1)} %slice.18), channel_id=1, source_target_pairs={{0,4},{1,5},{2,6},{3,7},{4,0},{5,1},{6,2},{7,3},{8,12},{9,13},{10,... | collective-permute-start | bytes 393224 | tf_op jit(solution)/shard_map/ppermute | solution.py:385
  38.0 1.6 %collective-permute-done.8.refs_4_ = bf16[128,512]{1,0:T(8,128)(2,1)S(1)} collective-permute-done((bf16[128,512]{1,0:T(8,128)(2,1)S(1)}, bf16[128,512]{1,0:T(8,128)(2,1)S(1)}, u32[]{:S(2)}, u32[]{:S(2)}) %collective-permute-start.8) | collective-permute-done | bytes 131104 | tf_op jit(solution)/shard_map/ppermute | solution.py:385
  39.6 1.5 %collective-permute-start.17 = (bf16[128,1024]{1,0:T(8,128)(2,1)S(1)}, bf16[128,1024]{1,0:T(8,128)(2,1)S(1)}, u32[]{:S(2)}, u32[]{:S(2)}) collective-permute-start(bf16[128,1024]{1,0:T(8,128)(2,1)S(1)} %collective-permute-done.15.refs_2_), channel_id=1, source_target_pairs={{0,4},{1,5},{2,6},{3,7},{4,0},{5,1},{6,2},{7,3},{8,12},{9,13},{10,... | collective-permute-start | bytes 786440 | tf_op jit(solution)/shard_map/ppermute | solution.py:385
  43.6 1.9 %collective-permute-done.13.refs_4_ = bf16[128,1024]{1,0:T(8,128)(2,1)S(1)} collective-permute-done((bf16[128,1024]{1,0:T(8,128)(2,1)S(1)}, bf16[128,1024]{1,0:T(8,128)(2,1)S(1)}, u32[]{:S(2)}, u32[]{:S(2)}) %collective-permute-start.13) | collective-permute-done | bytes 262176 | tf_op jit(solution)/shard_map/ppermute | solution.py:385
  46.2 3.1 %collective-permute-done.14.refs_1_ = bf16[128,1024]{1,0:T(8,128)(2,1)S(1)} collective-permute-done((bf16[128,1024]{1,0:T(8,128)(2,1)S(1)}, bf16[128,1024]{1,0:T(8,128)(2,1)S(1)}, u32[]{:S(2)}, u32[]{:S(2)}) %collective-permute-start.14) | collective-permute-done | bytes 262176 | tf_op jit(solution)/shard_map/ppermute | solution.py:385
  49.9 1.9 %collective-permute-done.18.b_ref = f32[128,1024]{1,0:T(8,128)S(1)} collective-permute-done((f32[128,1024]{1,0:T(8,128)S(1)}, f32[128,1024]{1,0:T(8,128)S(1)}, u32[]{:S(2)}, u32[]{:S(2)}) %collective-permute-start.18) | collective-permute-done | bytes 524320 | tf_op jit(solution)/shard_map/ppermute | solution.py:385
  51.9 3.4 %collective-permute-start.20 = (bf16[128,512]{1,0:T(8,128)(2,1)S(1)}, bf16[128,512]{1,0:T(8,128)(2,1)S(1)}, u32[]{:S(2)}, u32[]{:S(2)}) collective-permute-start(bf16[128,512]{1,0:T(8,128)(2,1)S(1)} %get-tuple-element.40.refs_0_), channel_id=1, source_target_pairs={{0,2},{1,3},{2,4},{3,5},{4,6},{5,7},{8,10},{9,11},{10,12},{11,13},... | collective-permute-start | bytes 393224 | tf_op jit(solution)/shard_map/ppermute | solution.py:385
  55.2 1.8 %collective-permute-start.19 = (bf16[128,512]{1,0:T(8,128)(2,1)S(1)}, bf16[128,512]{1,0:T(8,128)(2,1)S(1)}, u32[]{:S(2)}, u32[]{:S(2)}) collective-permute-start(bf16[128,512]{1,0:T(8,128)(2,1)S(1)} %get-tuple-element.40.refs_0_), channel_id=1, source_target_pairs={{0,1},{1,2},{2,3},{3,4},{4,5},{5,6},{6,7},{8,9},{9,10},{10,11},{11... | collective-permute-start | bytes 393224 | tf_op jit(solution)/shard_map/ppermute | solution.py:385
  58.4 5.6 %collective-permute-start.28 = (bf16[128,512]{1,0:T(8,128)(2,1)S(1)}, bf16[128,512]{1,0:T(8,128)(2,1)S(1)}, u32[]{:S(2)}, u32[]{:S(2)}) collective-permute-start(bf16[128,512]{1,0:T(8,128)(2,1)S(1)} %get-tuple-element.52.refs_0_), channel_id=1, source_target_pairs={{0,2},{1,3},{2,4},{3,5},{4,6},{5,7},{8,10},{9,11},{10,12},{11,13},... | collective-permute-start | bytes 393224 | tf_op jit(solution)/shard_map/ppermute | solution.py:385
  64.1 1.6 %fetch.1 = (bf16[128,4096]{1,0:T(8,128)(2,1)S(1)}, bf16[128,4096]{1,0:T(8,128)(2,1)S(1)}) custom-call(bf16[128,4096]{1,0:T(8,128)(2,1)} %bitcast.9, bf16[128,4096]{1,0:T(8,128)(2,1)} %bitcast.10), custom_call_target="tpu_custom_call" | custom-call | flops 1048576 | bytes 4194304 | tf_op jit(solution)/shard_map/fetch/pallas_call | solution.py:96
  68.0 4.8 %attend.2 = (bf16[128,2048]{1,0:T(8,128)(2,1)S(1)}, bf16[128,2048]{1,0:T(8,128)(2,1)S(1)}, f32[128,512]{1,0:T(8,128)S(1)}, bf16[128,512]{1,0:T(8,128)(2,1)S(1)}, f32[128,512]{1,0:T(8,128)S(1)}) custom-call(s32[1,8]{1,0:T(1,128)S(1)} %copy-done.2, bf16[128,4096]{1,0:T(8,128)(2,1)S(1)} %get-tuple-element.33.q_ref, ...), custom_call_target="tpu_custom_call" | custom-call | flops 2415919104 | bytes 4194304 | tf_op jit(solution)/shard_map/attend/pallas_call | solution.py:251
  72.9 3.2 %collective-permute-start.21 = (bf16[128,512]{1,0:T(8,128)(2,1)S(1)}, bf16[128,512]{1,0:T(8,128)(2,1)S(1)}, u32[]{:S(2)}, u32[]{:S(2)}) collective-permute-start(bf16[128,512]{1,0:T(8,128)(2,1)S(1)} %get-tuple-element.42), channel_id=1, source_target_pairs={{0,1},{1,0},{2,3},{3,2},{4,5},{5,4},{6,7},{7,6},{8,9},{9,8},{10,11... | collective-permute-start | bytes 393224 | tf_op jit(solution)/shard_map/ppermute | solution.py:385
  76.1 4.8 %attend.3 = (bf16[128,2048]{1,0:T(8,128)(2,1)S(1)}, bf16[128,2048]{1,0:T(8,128)(2,1)S(1)}, f32[128,512]{1,0:T(8,128)S(1)}, bf16[128,512]{1,0:T(8,128)(2,1)S(1)}, f32[128,512]{1,0:T(8,128)S(1)}) custom-call(s32[1,8]{1,0:T(1,128)S(1)} %copy-done.2, bf16[128,4096]{1,0:T(8,128)(2,1)S(1)} %get-tuple-element.33.q_ref, ...), custom_call_target="tpu_custom_call" | custom-call | flops 2415919104 | bytes 4194304 | tf_op jit(solution)/shard_map/attend/pallas_call | solution.py:251
  83.8 7.5 %collective-permute-done.22.refs_1_ = bf16[128,512]{1,0:T(8,128)(2,1)S(1)} collective-permute-done((bf16[128,512]{1,0:T(8,128)(2,1)S(1)}, bf16[128,512]{1,0:T(8,128)(2,1)S(1)}, u32[]{:S(2)}, u32[]{:S(2)}) %collective-permute-start.22) | collective-permute-done | bytes 131104 | tf_op jit(solution)/shard_map/ppermute | solution.py:385
  92.6 2.7 %finish.2 = (f32[128,4096]{1,0:T(8,128)S(1)}, bf16[128,4096]{1,0:T(8,128)(2,1)}, bf16[128,4096]{1,0:T(8,128)(2,1)}) custom-call(f32[128,512]{1,0:T(8,128)S(1)} %get-tuple-element.44.refs_0_, bf16[128,512]{1,0:T(8,128)(2,1)S(1)} %collective-permute-done.22.refs_1_, bf16[512,1024]{1,0:T(8,128)(2,1)S(1)} %get-tuple-element.46.refs_2_.refs_3_, ...), custom_call_target="tpu_custom_call" | custom-call | flops 536870912 | bytes 10485760 | tf_op jit(solution)/shard_map/finish/pallas_call | solution.py:359
  95.3 3.5 %collective-permute-done.30.refs_1_ = bf16[128,512]{1,0:T(8,128)(2,1)S(1)} collective-permute-done((bf16[128,512]{1,0:T(8,128)(2,1)S(1)}, bf16[128,512]{1,0:T(8,128)(2,1)S(1)}, u32[]{:S(2)}, u32[]{:S(2)}) %collective-permute-start.30) | collective-permute-done | bytes 131104 | tf_op jit(solution)/shard_map/ppermute | solution.py:385
  98.7 2.5 %finish.3 = bf16[128,4096]{1,0:T(8,128)(2,1)} custom-call(f32[128,512]{1,0:T(8,128)S(1)} %get-tuple-element.60.refs_0_, bf16[128,512]{1,0:T(8,128)(2,1)S(1)} %collective-permute-done.30.refs_1_, f32[128,4096]{1,0:T(8,128)S(1)} %get-tuple-element.62.refs_2_, bf16[512,1024]{1,0:T(8,128)(2,1)S(1)} %get-tuple-element.46.refs_2_.refs_3_, ...), custom_call_target="tpu_custom_call" | custom-call | flops 536870912 | bytes 10485760 | tf_op jit(solution)/shard_map/finish/pallas_call | solution.py:359
  (61 shorter events, 23.6 us)
Async XLA Ops:
  0.6 40.5 %collective-permute-start = (bf16[128,4096]{1,0:T(8,128)(2,1)}, bf16[128,4096]{1,0:T(8,128)(2,1)S(1)}, u32[]{:S(2)}, u32[]{:S(2)}) collective-permute-start(bf16[128,4096]{1,0:T(8,128)(2,1)} %bitcast.6), channel_id=1, source_target_pairs={{0,1},{1,0},{2,3},{3,2},{4,5},{5,4},{6,7},{7,6},{8,9},{9,8},{10,11... | collective-permute-start | bytes 3145736 | tf_op jit(solution)/shard_map/ppermute | solution.py:385
  1.2 11.8 %collective-permute-start.5 = (bf16[128,1024]{1,0:T(8,128)(2,1)}, bf16[128,1024]{1,0:T(8,128)(2,1)S(1)}, u32[]{:S(2)}, u32[]{:S(2)}) collective-permute-start(bf16[128,1024]{1,0:T(8,128)(2,1)} %refs_0_.1), channel_id=1, source_target_pairs={{0,8},{1,9},{2,10},{3,11},{4,12},{5,13},{6,14},{7,15},{8,16},{9,17... | collective-permute-start | bytes 786440 | tf_op jit(solution)/shard_map/ppermute | solution.py:385
  3.8 10.7 %collective-permute-start.2 = (bf16[128,1024]{1,0:T(8,128)(2,1)}, bf16[128,1024]{1,0:T(8,128)(2,1)S(1)}, u32[]{:S(2)}, u32[]{:S(2)}) collective-permute-start(bf16[128,1024]{1,0:T(8,128)(2,1)} %refs_0_.1), channel_id=1, source_target_pairs={{0,4},{1,5},{2,6},{3,7},{4,0},{5,1},{6,2},{7,3},{8,12},{9,13},{10,... | collective-permute-start | bytes 786440 | tf_op jit(solution)/shard_map/ppermute | solution.py:385
  5.3 10.6 %collective-permute-start.1 = (bf16[128,1024]{1,0:T(8,128)(2,1)}, bf16[128,1024]{1,0:T(8,128)(2,1)S(1)}, u32[]{:S(2)}, u32[]{:S(2)}) collective-permute-start(bf16[128,1024]{1,0:T(8,128)(2,1)} %refs_0_.1), channel_id=1, source_target_pairs={{0,2},{1,3},{2,0},{3,1},{4,6},{5,7},{6,4},{7,5},{8,10},{9,11},{10,... | collective-permute-start | bytes 786440 | tf_op jit(solution)/shard_map/ppermute | solution.py:385
  13.0 11.0 %collective-permute-start.10 = (bf16[128,1024]{1,0:T(8,128)(2,1)S(1)}, bf16[128,1024]{1,0:T(8,128)(2,1)S(1)}, u32[]{:S(2)}, u32[]{:S(2)}) collective-permute-start(bf16[128,1024]{1,0:T(8,128)(2,1)S(1)} %collective-permute-done.5.refs_1_), channel_id=1, source_target_pairs={{0,8},{1,9},{2,10},{3,11},{4,12},{5,13},{6,14},{7,15},{8,16},{9,17... | collective-permute-start | bytes 786440 | tf_op jit(solution)/shard_map/ppermute | solution.py:385
  13.0 12.6 %collective-permute-start.7 = (bf16[128,1024]{1,0:T(8,128)(2,1)S(1)}, bf16[128,1024]{1,0:T(8,128)(2,1)S(1)}, u32[]{:S(2)}, u32[]{:S(2)}) collective-permute-start(bf16[128,1024]{1,0:T(8,128)(2,1)S(1)} %collective-permute-done.5.refs_1_), channel_id=1, source_target_pairs={{0,4},{1,5},{2,6},{3,7},{4,0},{5,1},{6,2},{7,3},{8,12},{9,13},{10,... | collective-permute-start | bytes 786440 | tf_op jit(solution)/shard_map/ppermute | solution.py:385
  14.5 12.6 %collective-permute-start.6 = (bf16[128,1024]{1,0:T(8,128)(2,1)S(1)}, bf16[128,1024]{1,0:T(8,128)(2,1)S(1)}, u32[]{:S(2)}, u32[]{:S(2)}) collective-permute-start(bf16[128,1024]{1,0:T(8,128)(2,1)S(1)} %collective-permute-done.5.refs_1_), channel_id=1, source_target_pairs={{0,2},{1,3},{2,0},{3,1},{4,6},{5,7},{6,4},{7,5},{8,10},{9,11},{10,... | collective-permute-start | bytes 786440 | tf_op jit(solution)/shard_map/ppermute | solution.py:385
  16.0 18.8 %collective-permute-start.15 = (bf16[128,1024]{1,0:T(8,128)(2,1)S(1)}, bf16[128,1024]{1,0:T(8,128)(2,1)S(1)}, u32[]{:S(2)}, u32[]{:S(2)}) collective-permute-start(bf16[128,1024]{1,0:T(8,128)(2,1)S(1)} %collective-permute-done.1.refs_1_), channel_id=1, source_target_pairs={{0,24},{1,25},{2,26},{3,27},{4,28},{5,29},{6,30},{7,31},{8,0},{9,1... | collective-permute-start | bytes 786440 | tf_op jit(solution)/shard_map/ppermute | solution.py:385
  24.0 12.3 %collective-permute-start.12 = (bf16[128,1024]{1,0:T(8,128)(2,1)S(1)}, bf16[128,1024]{1,0:T(8,128)(2,1)S(1)}, u32[]{:S(2)}, u32[]{:S(2)}) collective-permute-start(bf16[128,1024]{1,0:T(8,128)(2,1)S(1)} %collective-permute-done.10.refs_1_), channel_id=1, source_target_pairs={{0,4},{1,5},{2,6},{3,7},{4,0},{5,1},{6,2},{7,3},{8,12},{9,13},{10,... | collective-permute-start | bytes 786440 | tf_op jit(solution)/shard_map/ppermute | solution.py:385
  31.7 6.4 %collective-permute-start.9 = (bf16[128,512]{1,0:T(8,128)(2,1)S(1)}, bf16[128,512]{1,0:T(8,128)(2,1)S(1)}, u32[]{:S(2)}, u32[]{:S(2)}) collective-permute-start(bf16[128,512]{1,0:T(8,128)(2,1)S(1)} %slice.19), channel_id=1, source_target_pairs={{0,2},{1,3},{2,0},{3,1},{4,6},{5,7},{6,4},{7,5},{8,10},{9,11},{10,... | collective-permute-start | bytes 393224 | tf_op jit(solution)/shard_map/ppermute | solution.py:385
  34.8 8.8 %collective-permute-start.11 = (bf16[128,1024]{1,0:T(8,128)(2,1)S(1)}, bf16[128,1024]{1,0:T(8,128)(2,1)S(1)}, u32[]{:S(2)}, u32[]{:S(2)}) collective-permute-start(bf16[128,1024]{1,0:T(8,128)(2,1)S(1)} %collective-permute-done.10.refs_1_), channel_id=1, source_target_pairs={{0,2},{1,3},{2,0},{3,1},{4,6},{5,7},{6,4},{7,5},{8,10},{9,11},{10,... | collective-permute-start | bytes 786440 | tf_op jit(solution)/shard_map/ppermute | solution.py:385
  36.3 9.3 %collective-permute-start.13 = (bf16[128,1024]{1,0:T(8,128)(2,1)S(1)}, bf16[128,1024]{1,0:T(8,128)(2,1)S(1)}, u32[]{:S(2)}, u32[]{:S(2)}) collective-permute-start(bf16[128,1024]{1,0:T(8,128)(2,1)S(1)} %collective-permute-done.12.refs_3_), channel_id=1, source_target_pairs={{0,2},{1,3},{2,0},{3,1},{4,6},{5,7},{6,4},{7,5},{8,10},{9,11},{10,... | collective-permute-start | bytes 786440 | tf_op jit(solution)/shard_map/ppermute | solution.py:385
  38.0 8.2 %collective-permute-start.16 = (bf16[128,1024]{1,0:T(8,128)(2,1)S(1)}, bf16[128,1024]{1,0:T(8,128)(2,1)S(1)}, u32[]{:S(2)}, u32[]{:S(2)}) collective-permute-start(bf16[128,1024]{1,0:T(8,128)(2,1)S(1)} %collective-permute-done.2.refs_2_), channel_id=1, source_target_pairs={{0,24},{1,25},{2,26},{3,27},{4,28},{5,29},{6,30},{7,31},{8,0},{9,1... | collective-permute-start | bytes 786440 | tf_op jit(solution)/shard_map/ppermute | solution.py:385
  39.6 6.6 %collective-permute-start.17 = (bf16[128,1024]{1,0:T(8,128)(2,1)S(1)}, bf16[128,1024]{1,0:T(8,128)(2,1)S(1)}, u32[]{:S(2)}, u32[]{:S(2)}) collective-permute-start(bf16[128,1024]{1,0:T(8,128)(2,1)S(1)} %collective-permute-done.15.refs_2_), channel_id=1, source_target_pairs={{0,4},{1,5},{2,6},{3,7},{4,0},{5,1},{6,2},{7,3},{8,12},{9,13},{10,... | collective-permute-start | bytes 786440 | tf_op jit(solution)/shard_map/ppermute | solution.py:385
  41.2 8.2 %collective-permute-start.14 = (bf16[128,1024]{1,0:T(8,128)(2,1)S(1)}, bf16[128,1024]{1,0:T(8,128)(2,1)S(1)}, u32[]{:S(2)}, u32[]{:S(2)}) collective-permute-start(bf16[128,1024]{1,0:T(8,128)(2,1)S(1)} %collective-permute-done.10.refs_1_), channel_id=1, source_target_pairs={{0,8},{1,9},{2,10},{3,11},{4,12},{5,13},{6,14},{7,15},{8,16},{9,17... | collective-permute-start | bytes 786440 | tf_op jit(solution)/shard_map/ppermute | solution.py:385
  51.9 6.5 %collective-permute-start.20 = (bf16[128,512]{1,0:T(8,128)(2,1)S(1)}, bf16[128,512]{1,0:T(8,128)(2,1)S(1)}, u32[]{:S(2)}, u32[]{:S(2)}) collective-permute-start(bf16[128,512]{1,0:T(8,128)(2,1)S(1)} %get-tuple-element.40.refs_0_), channel_id=1, source_target_pairs={{0,2},{1,3},{2,4},{3,5},{4,6},{5,7},{8,10},{9,11},{10,12},{11,13},... | collective-permute-start | bytes 393224 | tf_op jit(solution)/shard_map/ppermute | solution.py:385
  57.0 35.5 %collective-permute-start.26 = (bf16[512,1024]{1,0:T(8,128)(2,1)S(1)}, bf16[512,1024]{1,0:T(8,128)(2,1)S(1)}, u32[]{:S(2)}, u32[]{:S(2)}) collective-permute-start(bf16[512,1024]{1,0:T(8,128)(2,1)S(1)} %get-tuple-element.49.refs_5_.refs_6_), channel_id=1, source_target_pairs={{0,1},{1,0},{2,3},{3,2},{4,5},{5,4},{6,7},{7,6},{8,9},{9,8},{10,11... | collective-permute-start | bytes 3145736 | tf_op jit(solution)/shard_map/ppermute | solution.py:385
  57.8 34.7 %collective-permute-start.25 = (bf16[512,1024]{1,0:T(8,128)(2,1)S(1)}, bf16[512,1024]{1,0:T(8,128)(2,1)S(1)}, u32[]{:S(2)}, u32[]{:S(2)}) collective-permute-start(bf16[512,1024]{1,0:T(8,128)(2,1)S(1)} %get-tuple-element.48.refs_4_.refs_5_), channel_id=1, source_target_pairs={{0,1},{1,0},{2,3},{3,2},{4,5},{5,4},{6,7},{7,6},{8,9},{9,8},{10,11... | collective-permute-start | bytes 3145736 | tf_op jit(solution)/shard_map/ppermute | solution.py:385
  57.9 34.6 %collective-permute-start.24 = (bf16[512,1024]{1,0:T(8,128)(2,1)S(1)}, bf16[512,1024]{1,0:T(8,128)(2,1)S(1)}, u32[]{:S(2)}, u32[]{:S(2)}) collective-permute-start(bf16[512,1024]{1,0:T(8,128)(2,1)S(1)} %get-tuple-element.47.refs_3_.refs_4_), channel_id=1, source_target_pairs={{0,1},{1,0},{2,3},{3,2},{4,5},{5,4},{6,7},{7,6},{8,9},{9,8},{10,11... | collective-permute-start | bytes 3145736 | tf_op jit(solution)/shard_map/ppermute | solution.py:385
  58.4 34.2 %collective-permute-start.23 = (bf16[512,1024]{1,0:T(8,128)(2,1)S(1)}, bf16[512,1024]{1,0:T(8,128)(2,1)S(1)}, u32[]{:S(2)}, u32[]{:S(2)}) collective-permute-start(bf16[512,1024]{1,0:T(8,128)(2,1)S(1)} %get-tuple-element.46.refs_2_.refs_3_), channel_id=1, source_target_pairs={{0,1},{1,0},{2,3},{3,2},{4,5},{5,4},{6,7},{7,6},{8,9},{9,8},{10,11... | collective-permute-start | bytes 3145736 | tf_op jit(solution)/shard_map/ppermute | solution.py:385
  58.4 8.1 %collective-permute-start.28 = (bf16[128,512]{1,0:T(8,128)(2,1)S(1)}, bf16[128,512]{1,0:T(8,128)(2,1)S(1)}, u32[]{:S(2)}, u32[]{:S(2)}) collective-permute-start(bf16[128,512]{1,0:T(8,128)(2,1)S(1)} %get-tuple-element.52.refs_0_), channel_id=1, source_target_pairs={{0,2},{1,3},{2,4},{3,5},{4,6},{5,7},{8,10},{9,11},{10,12},{11,13},... | collective-permute-start | bytes 393224 | tf_op jit(solution)/shard_map/ppermute | solution.py:385
  72.9 8.1 %collective-permute-start.21 = (bf16[128,512]{1,0:T(8,128)(2,1)S(1)}, bf16[128,512]{1,0:T(8,128)(2,1)S(1)}, u32[]{:S(2)}, u32[]{:S(2)}) collective-permute-start(bf16[128,512]{1,0:T(8,128)(2,1)S(1)} %get-tuple-element.42), channel_id=1, source_target_pairs={{0,1},{1,0},{2,3},{3,2},{4,5},{5,4},{6,7},{7,6},{8,9},{9,8},{10,11... | collective-permute-start | bytes 393224 | tf_op jit(solution)/shard_map/ppermute | solution.py:385
  82.4 8.9 %collective-permute-start.22 = (bf16[128,512]{1,0:T(8,128)(2,1)S(1)}, bf16[128,512]{1,0:T(8,128)(2,1)S(1)}, u32[]{:S(2)}, u32[]{:S(2)}) collective-permute-start(bf16[128,512]{1,0:T(8,128)(2,1)S(1)} %get-tuple-element.45), channel_id=1, source_target_pairs={{2,0},{3,1},{4,2},{5,3},{6,4},{7,5},{10,8},{11,9},{12,10},{13,11},... | collective-permute-start | bytes 393224 | tf_op jit(solution)/shard_map/ppermute | solution.py:385
  91.3 7.5 %collective-permute-start.30 = (bf16[128,512]{1,0:T(8,128)(2,1)S(1)}, bf16[128,512]{1,0:T(8,128)(2,1)S(1)}, u32[]{:S(2)}, u32[]{:S(2)}) collective-permute-start(bf16[128,512]{1,0:T(8,128)(2,1)S(1)} %get-tuple-element.61), channel_id=1, source_target_pairs={{2,0},{3,1},{4,2},{5,3},{6,4},{7,5},{10,8},{11,9},{12,10},{13,11},... | collective-permute-start | bytes 393224 | tf_op jit(solution)/shard_map/ppermute | solution.py:385
  (10 other events, 93.1 us)
